TPU v7x, 128 devices: a whole 4x4x4 slice. The times are simulated.
128 devices in a mesh: dp: 16 (over z, x_lo, core), mp: 8 (over x_hi, y).
Axes of the slice: x: 4 (x_hi: 2, x_lo: 2; x = x_hi * 2 + x_lo), y: 4, z: 4, core: 2. Of those that a mesh axis runs over, the one named last changes fastest.
Arguments:
- master: float32 [8192, 5120], P('dp', 'mp'), may hold values from -60 to 60
- moment_first: float32 [8192, 5120], P('dp', 'mp'), may hold values from -0.06 to 0.06
- moment_second: float32 [8192, 5120], P('dp', 'mp'), may hold values from 1e-05 to 0.001
- gradients: float32 [8192, 5120], P('dp', 'mp'), may hold values from -0.2 to 0.2
- step_count: int32 [1], replicated, may hold values from 1 to 10
- tensor_rows: int32 [24], replicated, may hold values from 1 to 1280, 8192 in all
- decay_mask: int32 [24], replicated, may hold values 0 or 1
Outputs:
- new_master: float32 [8192, 5120], P('dp', 'mp')
- new_first: float32 [8192, 5120], P('dp', 'mp')
- new_second: float32 [8192, 5120], P('dp', 'mp')
- compute_weights: bfloat16 [8192, 5120], P(None, 'mp')
Inputs may be any that keep to these rules, and one draw needn't show every extreme that they name: `tensor_rows`: the rows sum to 8192; the largest tensor has 1280 rows.
All inputs are finite; a program needn't handle non-finite values.
Results may differ from a plain program's by a relative error of at most 0.0004.
Values may be sent and summed in bfloat16 or wider, within the bound.
A program may use at most 128 MiB of HBM per device.

v0:
```python
import jax
import jax.numpy as jnp
from jax import lax
from jax.sharding import PartitionSpec as P

beta_first = 0.9
beta_second = 0.999
adam_epsilon = 1e-06
decay_rate = 0.3
learn_rate = 0.3
norm_epsilon = 1e-06


def copy_for_each(x, axis):
    size = lax.axis_size(axis)
    return lax.all_to_all(jnp.broadcast_to(x[None], (size, *x.shape)), axis, 0, 0, tiled=True)


def over_copies(x, axis):
    everything = copy_for_each(x, axis)
    return jnp.sum(everything, axis=0)


def together(arrays, axis):
    flat, at, gathered = (jnp.concatenate([a.reshape(-1) for a in arrays]), 0, [])
    subtotal = over_copies(flat, axis)
    for a in arrays:
        gathered.append(subtotal[at : at + a.size].reshape(a.shape))
        at += a.size
    return tuple(gathered)


def membership(first_row, count, offsets, tensor_rows):
    row_ids = first_row + jnp.arange(count, dtype=jnp.int32)
    inside = (row_ids[None, :] >= offsets[:, None]) & (
        row_ids[None, :] < (offsets + tensor_rows)[:, None]
    )
    return inside.astype(jnp.float32)


def local(master, moment_first, moment_second, gradients, step_count, tensor_rows, decay_mask):
    rows_dev = master.shape[0]
    steps = step_count[0].astype(jnp.float32)
    new_first = beta_first * moment_first + (1.0 - beta_first) * gradients
    new_second = beta_second * moment_second + (1.0 - beta_second) * gradients * gradients
    fix_first = 1.0 - jnp.power(jnp.float32(beta_first), steps)
    fix_second = 1.0 - jnp.power(jnp.float32(beta_second), steps)
    offsets = jnp.cumsum(tensor_rows) - tensor_rows
    first_row = lax.axis_index("dp") * rows_dev
    member = membership(first_row, rows_dev, offsets, tensor_rows)
    mask_rows = jnp.dot(decay_mask.astype(jnp.float32), member, precision=lax.Precision.HIGHEST)
    update = new_first / fix_first / (jnp.sqrt(new_second / fix_second) + adam_epsilon)
    update = update + decay_rate * mask_rows[:, None] * master
    weight_part = jnp.dot(member, jnp.sum(master * master, axis=1), precision=lax.Precision.HIGHEST)
    update_part = jnp.dot(member, jnp.sum(update * update, axis=1), precision=lax.Precision.HIGHEST)
    column_sums = together((weight_part, update_part), "mp")
    weight_sq, update_sq = together((column_sums[0], column_sums[1]), "dp")
    ratio = jnp.sqrt(weight_sq) / (jnp.sqrt(update_sq) + norm_epsilon)
    ratio_rows = jnp.dot(ratio, member, precision=lax.Precision.HIGHEST)
    new_master = master - learn_rate * ratio_rows[:, None] * update
    compute_weights = lax.all_gather(new_master.astype(jnp.bfloat16), "dp", axis=0, tiled=True)
    return (new_master, new_first, new_second, compute_weights)


def solution(mesh):
    placed = (P("dp", "mp"), P("dp", "mp"), P("dp", "mp"), P("dp", "mp"), P(), P(), P())
    return jax.shard_map(
        local,
        mesh=mesh,
        in_specs=placed,
        out_specs=(P("dp", "mp"), P("dp", "mp"), P("dp", "mp"), P(None, "mp")),
        check_vma=False,
    )
```

profile of v0, /device:TPU:1, one launch (start us, length us, event | category | flops | bytes accessed | tf_op | source)
XLA Modules:
  0.0 118.2 jit_solution(8679923997820081381)
XLA Ops:
  7.2 0.0 all-gather.2.cloned.1.call-start
  8.0 0.7 copy.14
  8.7 0.1 reduce.2
  8.9 0.7 sub.18
  9.5 0.1 compare_and_fusion
  9.6 0.8 fusion.2
  10.4 0.0 copy-start
  10.4 5.1 %multiply_reduce_fusion = (f32[512]{0:T(512)S(1)}, f32[512,640]{1,0:T(8,128)S(1)}, f32[512,640]{1,0:T(8,128)}, f32[512,640]{1,0:T(8,128)}, f32[512]{0:T(512)S(1)}) fusion(f32[512,640]{1,0:T(8,128)} %param.7, f32[512]{0:T(512)S(1)} %broadcast_multiply_fusion.1, f32[]{:T(128)} %bitcast.4, f32[]{:T(128)} %bitcast.3, f32[512,640]{1,0:T(8,128)} %param.10, ...), kind=kLoop, calls=%fused_computation.3 | loop fusion | flops 5569536 | bytes 9181192 | tf_op jit(solution)/shard_map/reduce_sum | solution.py:55
  15.5 0.1 convolution_bitcast_fusion
  15.6 0.1 convolution_bitcast_fusion.1
  15.7 0.1 pad_maximum_fusion
  15.8 13.8 %all_to_all.12 = f32[8,1,48]{2,1,0:T(1,128)S(1)} all-to-all(f32[8,1,48]{2,1,0:T(1,128)S(1)} %broadcast_in_dim.4), channel_id=1, replica_groups=mesh['dp'=16,'mp'=8] {'mp'}, dimensions={0} | all-to-all | bytes 3072 | tf_op jit(solution)/shard_map/all_to_all | solution.py:16
  29.7 12.8 %all_to_all.13 = f32[16,1,48]{2,1,0:T(1,128)S(1)} all-to-all(f32[16,1,48]{2,1,0:T(1,128)S(1)} %broadcast_in_dim.5), channel_id=1, replica_groups=mesh['dp'=16,'mp'=8] {'dp'}, dimensions={0} | all-to-all | bytes 6144 | tf_op jit(solution)/shard_map/all_to_all | solution.py:16
  42.5 0.2 fusion.3
  42.7 0.0 copy-done
  42.7 1.5 %fusion.7 = (bf16[512,640]{1,0:T(8,128)(2,1)}, f32[512,640]{1,0:T(8,128)}) fusion(f32[512,640]{1,0:T(8,128)S(1)} %copy-done, f32[512,640]{1,0:T(8,128)S(1)} %get-tuple-element.7, f32[512]{0:T(512)S(1)} %broadcast_multiply_fusion), kind=kLoop, calls=%fused_computation.21 | loop fusion | flops 983040 | bytes 4589568 | tf_op jit(solution)/shard_map/convert_element_type | solution.py:61
  44.2 0.0 all-gather.2.cloned.1.call-update
  44.2 58.2 %all-gather.2.cloned.1.call-done = bf16[8192,640]{1,0:T(8,128)(2,1)} async-done(((bf16[512,640]{1,0:T(8,128)(2,1)}), bf16[8192,640]{1,0:T(8,128)(2,1)}) %all-gather.2.cloned.1.call-update) | async-done | bytes 10485776 | tf_op jit(solution)/shard_map/all_gather | solution.py:61
  102.4 9.0 %copy.19 = bf16[8192,640]{1,0:T(8,128)(2,1)} copy(bf16[8192,640]{1,0:T(8,128)(2,1)} %all-gather.2.cloned.1.call-done) | data formatting | bytes 20971520
  (8 shorter events, 0.1 us)
Async XLA Ops:
  7.2 95.2 %all-gather.2.cloned.1.call-start = ((), (), s32[]{:S(2)}) async-start(), calls=%async_computation.2 | async-start | bytes 11141120 | tf_op jit(solution)/shard_map/all_gather | solution.py:61
  10.4 32.3 %copy-start = (f32[512,640]{1,0:T(8,128)S(1)}, f32[512,640]{1,0:T(8,128)}, u32[]{:S(2)}) copy-start(f32[512,640]{1,0:T(8,128)} %param.7) | copy-start | bytes 3932164
Sparse Core Ops, SparseCore 0:
  44.3 58.0 all-gather.1
where the time goes:
time: 118 us
  waiting for transfers between devices  58.2 us (49%)
  blocking collectives  26.6 us (23%)
  between operations  14.8 us (13%)
  local copies, waits for them, and re-layouts  9.72 us (8%)
  other arithmetic  7.61 us (6%)
  matrix products  1.26 us (1%)
    all_gather x1, waiting for transfers between devices, local(): lax.all_gather(new_master.astype(jnp.bfloat16), 'dp', axis=0, tiled=True)  58.2 us
    all_to_all x2, blocking collectives, copy_for_each(): lax.all_to_all(jnp.broadcast_to(x[None], (size, *x.shape)), axis, 0, 0, t...  26.6 us
    unnamed x3, local copies, waits for them, and re-layouts  8.97 us
    reduce_sum x1, other arithmetic, local(): jnp.sum(update * update, axis=1)  5.08 us
  transfers between devices with their start and end apart: 1, of which 1 were waited for; matrix products, arithmetic and copies ran while one was open for 0% of the time, Pallas kernels for 0%

commit v1 on v0

--- a/solution.py
+++ b/solution.py
@@ -58,7 +58,12 @@
     ratio = jnp.sqrt(weight_sq) / (jnp.sqrt(update_sq) + norm_epsilon)
     ratio_rows = jnp.dot(ratio, member, precision=lax.Precision.HIGHEST)
     new_master = master - learn_rate * ratio_rows[:, None] * update
-    compute_weights = lax.all_gather(new_master.astype(jnp.bfloat16), "dp", axis=0, tiled=True)
+    compute_weights = jnp.concatenate(
+        lax.all_to_all(
+            jnp.stack([new_master.astype(jnp.bfloat16)] * lax.axis_size("dp")), "dp", 0, 0
+        ),
+        axis=0,
+    )
     return (new_master, new_first, new_second, compute_weights)
 
 

time: 118 us -> 168 us (1.42)
  blocking collectives: 26.6 us -> 147 us
  waiting for transfers between devices: 58.2 us -> 0 us
  between operations: 14.8 us -> 1.4 us
    all_to_all x0 -> x1, blocking collectives: none -> 120 us  [local(): lax.all_to_all(jnp.stack([new_master.astype(jnp.bfloat16)] * lax.axis_siz...]
    all_gather x1 -> x0, waiting for transfers between devices: 58.2 us -> none  [local(): lax.all_gather(new_master.astype(jnp.bfloat16), 'dp', axis=0, tiled=True)]
  transfers between devices with their start and end apart: 1 -> 0, of which waited for: 1 -> 0; matrix products, arithmetic and copies ran while one was open for 0% -> 0% of each run, Pallas kernels for 0% -> 0%
where the time goes in v1:
time: 168 us
  blocking collectives  147 us (88%)
  local copies, waits for them, and re-layouts  10.9 us (6%)
  other arithmetic  7.4 us (4%)
    all_to_all x1, blocking collectives, local(): lax.all_to_all(jnp.stack([new_master.astype(jnp.bfloat16)] * lax.axis_siz...  120 us
    all_to_all x2, blocking collectives, copy_for_each(): lax.all_to_all(jnp.broadcast_to(x[None], (size, *x.shape)), axis, 0, 0, t...  26.6 us
    unnamed x3, local copies, waits for them, and re-layouts  8.97 us
    reduce_sum x1, other arithmetic, local(): jnp.sum(update * update, axis=1)  5.08 us

profile of v1, /device:TPU:1, one launch (start us, length us, event | category | flops | bytes accessed | tf_op | source)
XLA Modules:
  0.0 168.0 jit_solution(8923153106042986510)
XLA Ops:
  1.4 0.7 copy.14
  2.2 0.1 reduce.2
  2.3 0.7 sub.18
  2.9 0.1 compare_and_fusion
  3.0 0.8 fusion.2
  3.8 0.0 copy-start
  3.8 5.1 %multiply_reduce_fusion = (f32[512]{0:T(512)S(1)}, f32[512,640]{1,0:T(8,128)S(1)}, f32[512,640]{1,0:T(8,128)}, f32[512,640]{1,0:T(8,128)}, f32[512]{0:T(512)S(1)}) fusion(f32[512,640]{1,0:T(8,128)} %param.7, f32[512]{0:T(512)S(1)} %broadcast_multiply_fusion.1, f32[]{:T(128)} %bitcast.4, f32[]{:T(128)} %bitcast.3, f32[512,640]{1,0:T(8,128)} %param.10, ...), kind=kLoop, calls=%fused_computation.3 | loop fusion | flops 5569536 | bytes 9181192 | tf_op jit(solution)/shard_map/reduce_sum | solution.py:55
  8.9 0.1 convolution_bitcast_fusion
  9.0 0.1 convolution_bitcast_fusion.1
  9.2 0.1 pad_maximum_fusion
  9.3 13.8 %all_to_all.17 = f32[8,1,48]{2,1,0:T(1,128)S(1)} all-to-all(f32[8,1,48]{2,1,0:T(1,128)S(1)} %broadcast_in_dim.4), channel_id=1, replica_groups=mesh['dp'=16,'mp'=8] {'mp'}, dimensions={0} | all-to-all | bytes 3072 | tf_op jit(solution)/shard_map/all_to_all | solution.py:16
  23.1 12.8 %all_to_all.18 = f32[16,1,48]{2,1,0:T(1,128)S(1)} all-to-all(f32[16,1,48]{2,1,0:T(1,128)S(1)} %broadcast_in_dim.5), channel_id=1, replica_groups=mesh['dp'=16,'mp'=8] {'dp'}, dimensions={0} | all-to-all | bytes 6144 | tf_op jit(solution)/shard_map/all_to_all | solution.py:16
  35.9 0.2 fusion.3
  36.1 0.0 copy-done
  36.1 1.3 fusion.7
  37.4 1.2 stack.2
  38.6 120.5 %all_to_all.19 = bf16[16,512,640]{2,1,0:T(8,128)(2,1)} all-to-all(bf16[16,512,640]{2,1,0:T(8,128)(2,1)S(1)} %stack.2), channel_id=1, replica_groups=mesh['dp'=16,'mp'=8] {'dp'}, dimensions={0} | all-to-all | bytes 20971520 | tf_op jit(solution)/shard_map/all_to_all | solution.py:62
  159.1 9.0 %copy.19 = bf16[8192,640]{1,0:T(8,128)(2,1)} copy(bf16[8192,640]{1,0:T(8,128)(2,1)} %bitcast.26) | data formatting | bytes 20971520
  (8 shorter events, 0.1 us)
Async XLA Ops:
  3.8 32.3 %copy-start = (f32[512,640]{1,0:T(8,128)S(1)}, f32[512,640]{1,0:T(8,128)}, u32[]{:S(2)}) copy-start(f32[512,640]{1,0:T(8,128)} %param.7) | copy-start | bytes 3932164
